TPU v7x, 256 devices: a whole 4x4x8 slice. The times are simulated.
256 devices in a mesh: freq: 8 (over x, core), rec: 32 (over z, y).
Axes of the slice: x: 4, y: 4, z: 8, core: 2. Of those that a mesh axis runs over, the one named last changes fastest.
Arguments:
- response_real: float32 [96, 1536, 1536], P('freq', 'rec'), may hold values from -0.109375 to 0.109375
- response_imaginary: float32 [96, 1536, 1536], P('freq', 'rec'), may hold values from -0.109375 to 0.109375
- focus: float32 [1536, 96, 128], P('rec', 'freq'), may hold values from -6 to 6
- initial: float32 [1536, 96, 128], P('rec', 'freq'), may hold values from -6 to 6
- onset: int32 [1536, 64], P('rec'), may hold values from 24 to 167
Outputs:
- focus_next: float32 [1536, 96, 128], P('rec', 'freq')
All inputs are finite; a program needn't handle non-finite values.
Results may differ from a plain program's by a relative error of at most 0.0003.
Values sent between devices are 32-bit elements; how exact they have to be, the bound alone decides.
No kernel may reach another device: no remote copies, remote signals or barrier semaphores. Data moves between devices by JAX's collectives and lax.ppermute only.
A program may use at most 128 MiB of HBM per device.

v0:
```python
import math
import jax
import jax.numpy as jnp
from jax import lax
from jax.sharding import Mesh
from jax.sharding import PartitionSpec as P

REC = ("rec_0", "rec_1")


def sum_by_axis(total, axes):
    for axis in axes:
        total = lax.psum_scatter(total, axis, scatter_dimension=0, tiled=True)
    return total


def tables(freqs):
    samples = 2 * freqs
    order = lax.iota(jnp.int32, freqs)
    sample = lax.iota(jnp.int32, samples)
    phase = order[:, None] * sample[None, :] % samples
    phases = 2.0 * math.pi / samples * phase.astype(jnp.float32)
    cosine = jnp.cos(phases)
    sine = jnp.sin(phases)
    factor = jnp.where(order == 0, 1.0, 2.0).astype(jnp.float32)[:, None] / samples
    inverse = jnp.stack([factor * cosine, -factor * sine])
    forward = jnp.stack([cosine, -sine])
    return (inverse, forward, sample)


def window(spectrum, onset):
    count, freqs, width = spectrum.shape
    half = width // 2
    inverse, forward, sample = tables(freqs)
    split = spectrum.reshape(count, freqs, 2, half)
    traces = jnp.einsum("nkcp,ckt->ntp", split, inverse, precision=lax.Precision.HIGHEST)
    keep = sample[None, :, None] < onset[:, None, :]
    clipped = jnp.where(keep, traces, 0.0)
    back = jnp.einsum("ntp,ckt->nkcp", clipped, forward, precision=lax.Precision.HIGHEST)
    return back.reshape(count, freqs, width)


def adjoint_terms(real_part, imag_part, values):
    half = values.shape[2] // 2
    first = jnp.einsum("frs,rfq->sfq", real_part, values, precision=lax.Precision.HIGHEST)
    second = jnp.einsum("frs,rfq->sfq", imag_part, values, precision=lax.Precision.HIGHEST)
    return jnp.concatenate(
        [first[..., :half] + second[..., half:], first[..., half:] - second[..., :half]], axis=2
    )


def forward_terms(real_part, imag_part, values):
    half = values.shape[2] // 2
    first = jnp.einsum("frs,sfq->rfq", real_part, values, precision=lax.Precision.HIGHEST)
    second = jnp.einsum("frs,sfq->rfq", imag_part, values, precision=lax.Precision.HIGHEST)
    return jnp.concatenate(
        [first[..., :half] - second[..., half:], first[..., half:] + second[..., :half]], axis=2
    )


def onset_rows(onset):
    owned = onset.shape[0] // lax.axis_size("freq")
    return lax.dynamic_slice_in_dim(onset, lax.axis_index("freq") * owned, owned, 0)


def iterate(response_real, response_imaginary, values, onset):
    local_onset = onset_rows(onset)
    real_cols = response_real
    imag_cols = response_imaginary
    partial_sum = sum_by_axis(adjoint_terms(real_cols, imag_cols, values), REC)
    turned = lax.all_to_all(partial_sum, "freq", split_axis=0, concat_axis=1, tiled=True)
    windowed = window(turned, local_onset)
    returned = lax.all_to_all(windowed, "freq", split_axis=1, concat_axis=0, tiled=True)
    real_cols = response_real
    imag_cols = response_imaginary
    forward = forward_terms(real_cols, imag_cols, lax.all_gather(returned, REC, axis=0, tiled=True))
    receiver_side = lax.all_to_all(forward, "freq", split_axis=0, concat_axis=1, tiled=True)
    clipped = window(receiver_side, local_onset)
    return lax.all_to_all(clipped, "freq", split_axis=1, concat_axis=0, tiled=True)


def on_device(response_real, response_imaginary, focus, initial, onset):
    real_used, imag_used = (response_real, response_imaginary)
    update = iterate(real_used, imag_used, focus, onset)
    return initial - update


def solution(mesh):
    finer = Mesh(mesh.devices.reshape(mesh.shape["freq"], 8, 4), ("freq", "rec_0", "rec_1"))
    in_specs = (
        P("freq", REC, None),
        P("freq", REC, None),
        P(REC, "freq", None),
        P(REC, "freq", None),
        P(REC, None),
    )
    out_specs = P(REC, "freq", None)
    return jax.shard_map(
        on_device, mesh=finer, in_specs=in_specs, out_specs=out_specs, check_vma=False
    )
```

profile of v0, /device:TPU:1, one launch (start us, length us, event | category | flops | bytes accessed | tf_op | source)
XLA Modules:
  0.0 388.9 jit_solution(16803704345804091583)
XLA Ops:
  6.5 2.0 copy-done
  8.5 8.9 %convolution_bitcast_fusion = f32[1536,12,128]{0,2,1:T(8,128)S(1)} fusion(f32[48,12,128]{2,0,1:T(8,128)} %param.7, f32[12,48,1536]{2,1,0:T(8,128)S(1)} %copy-done), kind=kOutput, calls=%fused_computation.1 | convolution fusion | flops 1358954496 | bytes 13271040 | tf_op jit(solution)/shard_map/frs,rfq->sfq/dot_general | solution.py:46
  17.5 8.0 %convolution_bitcast_fusion.1 = f32[1536,12,128]{0,2,1:T(8,128)S(1)} fusion(f32[48,12,128]{2,0,1:T(8,128)S(1)} %copy-done.4, f32[12,48,1536]{2,1,0:T(8,128)S(1)} %copy-done.2), kind=kOutput, calls=%fused_computation.2 | convolution fusion | flops 1358954496 | bytes 13271040 | tf_op jit(solution)/shard_map/frs,rfq->sfq/dot_general | solution.py:45
  25.5 3.5 slice_add_fusion
  29.0 7.3 %pad_maximum_fusion = f32[1536,12,128]{0,2,1:T(8,128)} fusion(f32[1536,12,64]{0,2,1:T(8,128)} %get-tuple-element.6, f32[1536,12,64]{0,2,1:T(8,128)S(1)} %get-tuple-element.5), kind=kLoop, calls=%fused_computation | loop fusion | flops 2359296 | bytes 18874368 | tf_op jit(solution)/shard_map/concatenate | solution.py:47
  36.3 9.6 %copy.44 = f32[1536,1536]{1,0:T(8,128)} copy(f32[1536,1536]{0,1:T(8,128)} %bitcast.81) | data formatting | bytes 18874368
  46.0 108.7 %reduce-scatter.7.cloned.1.call-done = f32[192,1536]{1,0:T(8,128)} async-done(((f32[1536,1536]{1,0:T(8,128)}), f32[192,1536]{1,0:T(8,128)}) %reduce-scatter.7.cloned.1.call-update) | async-done | bytes 1179664
  154.6 2.9 copy.45
  157.5 3.4 copy.15
  162.8 24.4 %reduce-scatter.5.cloned.1.call-done = f32[48,12,128]{2,1,0:T(8,128)} async-done(((f32[192,12,128]{2,1,0:T(8,128)}), f32[48,12,128]{2,1,0:T(8,128)}) %reduce-scatter.5.cloned.1.call-update) | async-done | bytes 294928 | tf_op jit(solution)/shard_map/reduce_scatter | solution.py:13
  187.2 5.7 %all-to-all-start = ((f32[48,12,128]{2,1,0:T(8,128)}), f32[48,12,128]{2,1,0:T(8,128)}, u32[]{:S(2)}, u32[]{:S(2)}) async-start(f32[48,12,128]{2,1,0:T(8,128)} %reduce-scatter.5.cloned.1.call-done), calls=%async_computation.1 | async-start | bytes 786432 | tf_op jit(solution)/shard_map/all_to_all | solution.py:71
  194.0 6.7 %all-to-all-done = f32[48,12,128]{2,1,0:T(8,128)} async-done(((f32[48,12,128]{2,1,0:T(8,128)}), f32[48,12,128]{2,1,0:T(8,128)}, u32[]{:S(2)}, u32[]{:S(2)}) %all-to-all-start) | async-done | bytes 294944 | tf_op jit(solution)/shard_map/all_to_all | solution.py:71
  202.5 2.2 reshape.140
  204.6 2.3 fusion.1
  209.2 1.9 copy.20
  211.1 12.6 %all_to_all.66 = f32[6,96,128]{2,0,1:T(8,128)S(1)} all-to-all(f32[6,96,128]{2,0,1:T(8,128)} %copy.20), channel_id=1, replica_groups=mesh['freq'=8,'rec_0'=8,'rec_1'=4] {'freq'}, dimensions={1} | all-to-all | bytes 589824 | tf_op jit(solution)/shard_map/all_to_all | solution.py:73
  226.3 100.8 %all-gather.2.cloned.1.call-done = f32[1536,12,128]{2,0,1:T(8,128)} async-done(((f32[48,12,128]{2,0,1:T(8,128)}), f32[1536,12,128]{2,0,1:T(8,128)}) %all-gather.2.cloned.1.call-update) | async-done | bytes 9437200 | tf_op jit(solution)/shard_map/all_gather | solution.py:76
  327.1 9.3 %convolution_bitcast_fusion.6 = f32[48,12,128]{2,0,1:T(8,128)S(1)} fusion(f32[1536,12,128]{2,0,1:T(8,128)} %all-gather.2.cloned.1.call-done, f32[12,48,1536]{2,1,0:T(8,128)S(1)} %copy-done), kind=kOutput, calls=%fused_computation.9 | convolution fusion | flops 1358954496 | bytes 13271040 | tf_op jit(solution)/shard_map/frs,sfq->rfq/dot_general | solution.py:55
  336.4 6.0 %convolution_bitcast_fusion.7 = f32[48,12,128]{2,0,1:T(8,128)S(1)} fusion(f32[1536,12,128]{2,0,1:T(8,128)S(1)} %copy-done.1, f32[12,48,1536]{2,1,0:T(8,128)S(1)} %copy-done.3), kind=kOutput, calls=%fused_computation.10 | convolution fusion | flops 1358954496 | bytes 13271040 | tf_op jit(solution)/shard_map/frs,sfq->rfq/dot_general | solution.py:54
  342.9 13.5 %all_to_all.67 = f32[48,12,128]{2,1,0:T(8,128)S(1)} all-to-all(f32[48,12,128]{2,1,0:T(8,128)S(1)} %copy.23), channel_id=1, replica_groups=mesh['freq'=8,'rec_0'=8,'rec_1'=4] {'freq'}, dimensions={0} | all-to-all | bytes 589824 | tf_op jit(solution)/shard_map/all_to_all | solution.py:77
  357.2 2.2 reshape.142
  359.3 2.3 fusion.3
  363.9 1.9 copy.28
  365.8 12.3 %all_to_all.68 = f32[6,96,128]{2,0,1:T(8,128)S(1)} all-to-all(f32[6,96,128]{2,0,1:T(8,128)} %copy.28), channel_id=1, replica_groups=mesh['freq'=8,'rec_0'=8,'rec_1'=4] {'freq'}, dimensions={1} | all-to-all | bytes 589824 | tf_op jit(solution)/shard_map/all_to_all | solution.py:79
  (34 shorter events, 17.3 us)
Async XLA Ops:
  6.5 2.0 copy-start
  6.5 148.1 %reduce-scatter.7.cloned.1.call-start = ((), (), s32[]{:S(2)}) async-start(), calls=%async_computation.8 | async-start | bytes 10616832
  8.5 8.9 %copy-start.2 = (f32[12,48,1536]{2,1,0:T(8,128)S(1)}, f32[12,48,1536]{2,1,0:T(8,128)}, u32[]{:S(2)}) copy-start(f32[12,48,1536]{2,1,0:T(8,128)} %param.5) | copy-start | bytes 10616836
  8.5 9.0 %copy-start.4 = (f32[48,12,128]{2,0,1:T(8,128)S(1)}, f32[48,12,128]{2,0,1:T(8,128)}, u32[]{:S(2)}) copy-start(f32[48,12,128]{2,0,1:T(8,128)} %param.7) | copy-start | bytes 884740
  45.9 141.2 %reduce-scatter.5.cloned.1.call-start = ((), (), s32[]{:S(2)}) async-start(), calls=%async_computation.6 | async-start | bytes 1966080 | tf_op jit(solution)/shard_map/reduce_scatter | solution.py:13
  187.2 13.5 %all-to-all-start = ((f32[48,12,128]{2,1,0:T(8,128)}), f32[48,12,128]{2,1,0:T(8,128)}, u32[]{:S(2)}, u32[]{:S(2)}) async-start(f32[48,12,128]{2,1,0:T(8,128)} %reduce-scatter.5.cloned.1.call-done), calls=%async_computation.1 | async-start | bytes 786432 | tf_op jit(solution)/shard_map/all_to_all | solution.py:71
  192.9 134.2 %all-gather.2.cloned.1.call-start = ((), (), s32[]{:S(2)}) async-start(), calls=%async_computation.7 | async-start | bytes 9732096 | tf_op jit(solution)/shard_map/all_gather | solution.py:76
  327.1 9.3 %copy-start.1 = (f32[1536,12,128]{2,0,1:T(8,128)S(1)}, f32[1536,12,128]{2,0,1:T(8,128)}, u32[]{:S(2)}) copy-start(f32[1536,12,128]{2,0,1:T(8,128)} %all-gather.2.cloned.1.call-done) | copy-start | bytes 28311556
  327.1 9.3 %copy-start.3 = (f32[12,48,1536]{2,1,0:T(8,128)S(1)}, f32[12,48,1536]{2,1,0:T(8,128)}, u32[]{:S(2)}) copy-start(f32[12,48,1536]{2,1,0:T(8,128)} %param.5) | copy-start | bytes 10616836
Sparse Core Ops, SparseCore 0:
  46.0 108.5 reduce-scatter.6
  161.0 26.0 reduce-scatter.4
  226.4 100.6 all-gather.1
where the time goes:
time: 390 us; the launch traced here: 389 us
  waiting for transfers between devices  241 us (62%)
  matrix products  39.7 us (10%)
  blocking collectives  38.4 us (10%)
  local copies, waits for them, and re-layouts  36 us (9%)
  other arithmetic  15.2 us (4%)
  between operations  13.2 us (3%)
  starting transfers between devices  5.78 us (1%)
    unnamed x4, waiting for transfers between devices  109 us
    all_gather x1, waiting for transfers between devices, iterate(): lax.all_gather(returned, REC, axis=0, tiled=True)  101 us
    reduce_scatter x1, waiting for transfers between devices, sum_by_axis(): total = lax.psum_scatter(total, axis, scatter_dimension=0, tiled=True)  24.4 us
    unnamed x12, local copies, waits for them, and re-layouts  14.5 us
    all_to_all x1, blocking collectives, iterate(): lax.all_to_all(forward, 'freq', split_axis=0, concat_axis=1, tiled=True)  13.5 us
    all_to_all x1, blocking collectives, iterate(): lax.all_to_all(windowed, 'freq', split_axis=1, concat_axis=0, tiled=True)  12.6 us
    all_to_all x1, blocking collectives, iterate(): lax.all_to_all(clipped, 'freq', split_axis=1, concat_axis=0, tiled=True)  12.3 us
    dot_general x1, matrix products, forward_terms(): jnp.einsum('frs,sfq->rfq', imag_part, values, precision=lax.Precision.HIG...  9.26 us
  transfers between devices with their start and end apart: 4, of which 4 were waited for; matrix products, arithmetic and copies ran while one was open for 1% of the time, Pallas kernels for 0%

commit v1 on v0

--- a/solution.py
+++ b/solution.py
@@ -73,7 +73,13 @@
     returned = lax.all_to_all(windowed, "freq", split_axis=1, concat_axis=0, tiled=True)
     real_cols = response_real
     imag_cols = response_imaginary
-    forward = forward_terms(real_cols, imag_cols, lax.all_gather(returned, REC, axis=0, tiled=True))
+    forward = forward_terms(
+        real_cols,
+        imag_cols,
+        jnp.concatenate(
+            lax.all_to_all(jnp.stack([returned] * lax.axis_size(REC)), REC, 0, 0), axis=0
+        ),
+    )
     receiver_side = lax.all_to_all(forward, "freq", split_axis=0, concat_axis=1, tiled=True)
     clipped = window(receiver_side, local_onset)
     return lax.all_to_all(clipped, "freq", split_axis=1, concat_axis=0, tiled=True)

time: 390 us -> 516 us (1.32); the launches traced: 389 us -> 506 us
  blocking collectives: 38.4 us -> 252 us
  waiting for transfers between devices: 241 us -> 140 us
  local copies, waits for them, and re-layouts: 36 us -> 42.7 us
    all_to_all x0 -> x1, blocking collectives: none -> 214 us  [iterate(): lax.all_to_all(jnp.stack([returned] * lax.axis_size(REC)), REC, 0, 0)]
    all_gather x1 -> x0, waiting for transfers between devices: 101 us -> none  [iterate(): lax.all_gather(returned, REC, axis=0, tiled=True)]
    unnamed x4 -> x3, waiting for transfers between devices: 109 us -> 109 us
    unnamed x12 -> x10, local copies, waits for them, and re-layouts: 14.5 us -> 14.5 us
  transfers between devices with their start and end apart: 4 -> 3, of which waited for: 4 -> 3; matrix products, arithmetic and copies ran while one was open for 1% -> 1% of each run, Pallas kernels for 0% -> 0%
where the time goes in v1:
time: 516 us; the launch traced here: 506 us
  blocking collectives  252 us (49%)
  waiting for transfers between devices  140 us (27%)
  local copies, waits for them, and re-layouts  42.7 us (8%)
  matrix products  37 us (7%)
  other arithmetic  15.2 us (3%)
  between operations  13.8 us (3%)
  starting transfers between devices  5.77 us (1%)
    all_to_all x1, blocking collectives, iterate(): lax.all_to_all(jnp.stack([returned] * lax.axis_size(REC)), REC, 0, 0)  214 us
    unnamed x3, waiting for transfers between devices  109 us
    reduce_scatter x1, waiting for transfers between devices, sum_by_axis(): total = lax.psum_scatter(total, axis, scatter_dimension=0, tiled=True)  24.4 us
    unnamed x10, local copies, waits for them, and re-layouts  14.5 us
    all_to_all x1, blocking collectives, iterate(): lax.all_to_all(forward, 'freq', split_axis=0, concat_axis=1, tiled=True)  13.3 us
    all_to_all x1, blocking collectives, iterate(): lax.all_to_all(windowed, 'freq', split_axis=1, concat_axis=0, tiled=True)  12.6 us
    all_to_all x1, blocking collectives, iterate(): lax.all_to_all(clipped, 'freq', split_axis=1, concat_axis=0, tiled=True)  12.3 us
  transfers between devices with their start and end apart: 3, of which 3 were waited for; matrix products, arithmetic and copies ran while one was open for 1% of the time, Pallas kernels for 0%

profile of v1, /device:TPU:1, one launch (start us, length us, event | category | flops | bytes accessed | tf_op | source)
XLA Modules:
  0.0 506.3 jit_solution(5293982630117297760)
XLA Ops:
  6.5 2.0 copy-done
  8.5 8.9 %convolution_bitcast_fusion = f32[1536,12,128]{0,2,1:T(8,128)S(1)} fusion(f32[48,12,128]{2,0,1:T(8,128)} %param.7, f32[12,48,1536]{2,1,0:T(8,128)S(1)} %copy-done), kind=kOutput, calls=%fused_computation.1 | convolution fusion | flops 1358954496 | bytes 13271040 | tf_op jit(solution)/shard_map/frs,rfq->sfq/dot_general | solution.py:46
  17.5 8.3 %convolution_bitcast_fusion.1 = f32[1536,12,128]{0,2,1:T(8,128)S(1)} fusion(f32[48,12,128]{2,0,1:T(8,128)S(1)} %copy-done.3, f32[12,48,1536]{2,1,0:T(8,128)S(1)} %copy-done.1), kind=kOutput, calls=%fused_computation.2 | convolution fusion | flops 1358954496 | bytes 13271040 | tf_op jit(solution)/shard_map/frs,rfq->sfq/dot_general | solution.py:45
  25.8 3.5 slice_add_fusion
  29.3 7.3 %pad_maximum_fusion = f32[1536,12,128]{0,2,1:T(8,128)} fusion(f32[1536,12,64]{0,2,1:T(8,128)} %get-tuple-element.6, f32[1536,12,64]{0,2,1:T(8,128)S(1)} %get-tuple-element.5), kind=kLoop, calls=%fused_computation | loop fusion | flops 2359296 | bytes 18874368 | tf_op jit(solution)/shard_map/concatenate | solution.py:47
  36.6 9.6 %copy.45 = f32[1536,1536]{1,0:T(8,128)} copy(f32[1536,1536]{0,1:T(8,128)} %bitcast.84) | data formatting | bytes 18874368
  46.2 108.7 %reduce-scatter.7.cloned.1.call-done = f32[192,1536]{1,0:T(8,128)} async-done(((f32[1536,1536]{1,0:T(8,128)}), f32[192,1536]{1,0:T(8,128)}) %reduce-scatter.7.cloned.1.call-update) | async-done | bytes 1179664
  154.9 2.9 copy.46
  157.8 3.4 copy.15
  163.0 24.4 %reduce-scatter.5.cloned.1.call-done = f32[48,12,128]{2,1,0:T(8,128)} async-done(((f32[192,12,128]{2,1,0:T(8,128)}), f32[48,12,128]{2,1,0:T(8,128)}) %reduce-scatter.5.cloned.1.call-update) | async-done | bytes 294928 | tf_op jit(solution)/shard_map/reduce_scatter | solution.py:13
  187.4 5.7 %all-to-all-start = ((f32[48,12,128]{2,1,0:T(8,128)}), f32[48,12,128]{2,1,0:T(8,128)}, u32[]{:S(2)}, u32[]{:S(2)}) async-start(f32[48,12,128]{2,1,0:T(8,128)} %reduce-scatter.5.cloned.1.call-done), calls=%async_computation.1 | async-start | bytes 786432 | tf_op jit(solution)/shard_map/all_to_all | solution.py:71
  194.3 6.7 %all-to-all-done = f32[48,12,128]{2,1,0:T(8,128)} async-done(((f32[48,12,128]{2,1,0:T(8,128)}), f32[48,12,128]{2,1,0:T(8,128)}, u32[]{:S(2)}, u32[]{:S(2)}) %all-to-all-start) | async-done | bytes 294944 | tf_op jit(solution)/shard_map/all_to_all | solution.py:71
  202.7 2.2 reshape.146
  204.9 2.3 fusion.1
  211.4 12.6 %all_to_all.68 = f32[6,96,128]{2,0,1:T(8,128)S(1)} all-to-all(f32[6,96,128]{2,0,1:T(8,128)} %copy.20), channel_id=1, replica_groups=mesh['freq'=8,'rec_0'=8,'rec_1'=4] {'freq'}, dimensions={1} | all-to-all | bytes 589824 | tf_op jit(solution)/shard_map/all_to_all | solution.py:73
  226.5 2.0 stack.11
  228.5 213.9 %all_to_all.69 = f32[32,48,12,128]{3,1,2,0:T(8,128)} all-to-all(f32[32,48,12,128]{3,1,2,0:T(8,128)S(1)} %stack.11), channel_id=1, replica_groups=mesh['freq'=8,'rec_0'=8,'rec_1'=4] {'rec_0','rec_1'}, dimensions={0} | all-to-all | bytes 18874368 | tf_op jit(solution)/shard_map/all_to_all | solution.py:80
  442.4 4.6 copy.23
  447.1 6.0 %convolution_bitcast_fusion.6 = f32[48,12,128]{2,0,1:T(8,128)S(1)} fusion(f32[1536,12,128]{2,0,1:T(8,128)S(1)} %bitcast.82, f32[12,48,1536]{2,1,0:T(8,128)S(1)} %copy-done), kind=kOutput, calls=%fused_computation.9 | convolution fusion | flops 1358954496 | bytes 13271040 | tf_op jit(solution)/shard_map/frs,sfq->rfq/dot_general | solution.py:55
  453.1 6.3 %convolution_bitcast_fusion.7 = f32[48,12,128]{2,0,1:T(8,128)S(1)} fusion(f32[1536,12,128]{2,0,1:T(8,128)S(1)} %bitcast.83, f32[12,48,1536]{2,1,0:T(8,128)S(1)} %copy-done.2), kind=kOutput, calls=%fused_computation.10 | convolution fusion | flops 1358954496 | bytes 13271040 | tf_op jit(solution)/shard_map/frs,sfq->rfq/dot_general | solution.py:54
  459.9 13.3 %all_to_all.70 = f32[48,12,128]{2,1,0:T(8,128)S(1)} all-to-all(f32[48,12,128]{2,1,0:T(8,128)S(1)} %copy.24), channel_id=1, replica_groups=mesh['freq'=8,'rec_0'=8,'rec_1'=4] {'freq'}, dimensions={0} | all-to-all | bytes 589824 | tf_op jit(solution)/shard_map/all_to_all | solution.py:83
  474.0 2.2 reshape.149
  476.2 2.3 fusion.3
  482.7 12.3 %all_to_all.71 = f32[6,96,128]{2,0,1:T(8,128)S(1)} all-to-all(f32[6,96,128]{2,0,1:T(8,128)} %copy.29), channel_id=1, replica_groups=mesh['freq'=8,'rec_0'=8,'rec_1'=4] {'freq'}, dimensions={1} | all-to-all | bytes 589824 | tf_op jit(solution)/shard_map/all_to_all | solution.py:85
  (32 shorter events, 21.2 us)
Async XLA Ops:
  6.5 2.0 copy-start
  6.5 148.3 %reduce-scatter.7.cloned.1.call-start = ((), (), s32[]{:S(2)}) async-start(), calls=%async_computation.8 | async-start | bytes 10616832
  8.5 8.9 %copy-start.1 = (f32[12,48,1536]{2,1,0:T(8,128)S(1)}, f32[12,48,1536]{2,1,0:T(8,128)}, u32[]{:S(2)}) copy-start(f32[12,48,1536]{2,1,0:T(8,128)} %param.5) | copy-start | bytes 10616836
  8.5 9.0 %copy-start.3 = (f32[48,12,128]{2,0,1:T(8,128)S(1)}, f32[48,12,128]{2,0,1:T(8,128)}, u32[]{:S(2)}) copy-start(f32[48,12,128]{2,0,1:T(8,128)} %param.7) | copy-start | bytes 884740
  46.2 141.2 %reduce-scatter.5.cloned.1.call-start = ((), (), s32[]{:S(2)}) async-start(), calls=%async_computation.7 | async-start | bytes 1966080 | tf_op jit(solution)/shard_map/reduce_scatter | solution.py:13
  187.4 13.5 %all-to-all-start = ((f32[48,12,128]{2,1,0:T(8,128)}), f32[48,12,128]{2,1,0:T(8,128)}, u32[]{:S(2)}, u32[]{:S(2)}) async-start(f32[48,12,128]{2,1,0:T(8,128)} %reduce-scatter.5.cloned.1.call-done), calls=%async_computation.1 | async-start | bytes 786432 | tf_op jit(solution)/shard_map/all_to_all | solution.py:71
  447.1 6.0 %copy-start.2 = (f32[12,48,1536]{2,1,0:T(8,128)S(1)}, f32[12,48,1536]{2,1,0:T(8,128)}, u32[]{:S(2)}) copy-start(f32[12,48,1536]{2,1,0:T(8,128)} %param.5) | copy-start | bytes 10616836
Sparse Core Ops, SparseCore 0:
  46.3 108.5 reduce-scatter.6
  161.3 26.0 reduce-scatter.4
